TPU v7x, 32 devices: a whole 2x2x4 slice. The times are simulated.
32 devices in a mesh: rep: 1, fsdp: 32 (over z, y, x, core).
Axes of the slice: x: 2, y: 2, z: 4, core: 2. Of those that a mesh axis runs over, the one named last changes fastest.
Arguments:
- grads: bfloat16 [1, 24, 1280, 1280], P('rep', None, 'fsdp'), as said below
- group_counts: int32 [2], replicated, may hold values from 1 to 18, 24 in all
- owners: int32 [24], replicated, may hold values from 0 to 31, as said below
- left_stat: float32 [32, 1280, 1280], P('fsdp', 'rep'), may hold values from -4 to 4
- right_stat: float32 [32, 1280, 1280], P('fsdp', 'rep'), may hold values from -4 to 4
- left_root: bfloat16 [32, 1280, 1280], P('fsdp', 'rep'), as said below
- right_root: bfloat16 [32, 1280, 1280], P('fsdp', 'rep'), as said below
Outputs:
- left_new: float32 [32, 1280, 1280], P('fsdp', 'rep')
- right_new: float32 [32, 1280, 1280], P('fsdp', 'rep')
- update: bfloat16 [24, 1280, 1280], P(None, ('rep', 'fsdp'))
Inputs may be any that keep to these rules, and one draw needn't show every extreme that they name: `grads`: block gradients of every replica group, real-valued. `owners`: no slot is named by two blocks. `group_counts`: the counts add up to 24. `left_root`: Symmetric, with a positive diagonal of about 0.5 to 2, each entry within a small symmetric perturbation of that range, and off-diagonal entries much smaller than the diagonal. `right_root`: Symmetric, with a positive diagonal of about 0.5 to 2, each entry within a small symmetric perturbation of that range, and off-diagonal entries much smaller than the diagonal.
All inputs are finite; a program needn't handle non-finite values.
Results may differ from a plain program's by a relative error of at most 0.00065.
The roundings to bfloat16 on the way count: a program that leaves them out, or rounds other values in their place, can miss the bound.
Values may be sent and summed in bfloat16 or wider, within the bound.
No kernel may reach another device: no remote copies, remote signals or barrier semaphores. Data moves between devices by JAX's collectives and lax.ppermute only.
A program may use at most 128 MiB of HBM per device.

v0:
```python
import jax
import jax.numpy as jnp
from jax import lax
from jax.sharding import PartitionSpec as P

BETA = 0.95
EPSILON = 1e-06


def on_device(grads, group_counts, owners, left_stat, right_stat, left_root, right_root):
    slots = lax.axis_size("fsdp")
    width = left_stat.shape[2]
    half_rows = left_stat.shape[1]
    slot_ids = jnp.arange(slots, dtype=jnp.int32)
    placing = (owners[:, None] == slot_ids[None, :]).astype(jnp.bfloat16)
    local = grads[0]
    summed = lax.psum(local, "rep").astype(jnp.float32).astype(jnp.bfloat16)
    slotted = jnp.einsum("bs,brc->src", placing, summed, preferred_element_type=jnp.float32).astype(
        jnp.bfloat16
    )
    block = lax.all_to_all(slotted, "fsdp", split_axis=0, concat_axis=1, tiled=True)[0]
    first = lax.axis_index("rep") * half_rows
    mine = lax.dynamic_slice_in_dim(block, first, half_rows, 0)
    columns = lax.dynamic_slice_in_dim(block, first, half_rows, 1)
    coef = (1.0 - BETA) / width
    left_gram = jnp.dot(mine, block.T, preferred_element_type=jnp.float32)
    right_gram = lax.dot_general(
        columns, block, (((0,), (0,)), ((), ())), preferred_element_type=jnp.float32
    )
    left_new = BETA * left_stat[0] + coef * left_gram
    right_new = BETA * right_stat[0] + coef * right_gram
    whole_root = lax.all_gather(right_root, "rep", axis=1, tiled=True)[0]
    halfway = jnp.dot(left_root[0], block, preferred_element_type=jnp.float32).astype(jnp.bfloat16)
    precond = jnp.dot(halfway, whole_root, preferred_element_type=jnp.float32)
    ends = jnp.cumsum(group_counts)
    starts = ends - group_counts
    block_ids = jnp.arange(owners.shape[0], dtype=jnp.int32)
    member = (
        (block_ids[:, None] >= starts[None, :]) & (block_ids[:, None] < ends[None, :])
    ).astype(jnp.float32)
    owned_here = (owners == lax.axis_index("fsdp")).astype(jnp.float32)
    my_groups = jnp.sum(owned_here[:, None] * member, axis=0)
    mine_float = mine.astype(jnp.float32)
    grad_part = my_groups * jnp.sum(mine_float * mine_float)
    prec_part = my_groups * jnp.sum(precond * precond)
    grad_sq, prec_sq = lax.psum((grad_part, prec_part), ("rep", "fsdp"))
    ratio = jnp.sum(my_groups * jnp.sqrt((grad_sq + EPSILON) / (prec_sq + EPSILON)))
    scaled = (precond * ratio).astype(jnp.bfloat16)
    returned = lax.all_to_all(scaled[None], "fsdp", split_axis=1, concat_axis=0, tiled=True)
    update = jnp.einsum(
        "bs,srw->brw", placing, returned, preferred_element_type=jnp.float32
    ).astype(jnp.bfloat16)
    return (left_new[None], right_new[None], update)


def solution(mesh):
    in_specs = (
        P("rep", None, "fsdp", None),
        P(),
        P(),
        P("fsdp", "rep", None),
        P("fsdp", "rep", None),
        P("fsdp", "rep", None),
        P("fsdp", "rep", None),
    )
    out_specs = (P("fsdp", "rep", None), P("fsdp", "rep", None), P(None, ("rep", "fsdp"), None))
    return jax.shard_map(
        on_device, mesh=mesh, in_specs=in_specs, out_specs=out_specs, check_vma=False
    )
```

profile of v0, /device:TPU:0, one launch (start us, length us, event | category | flops | bytes accessed | tf_op | source)
XLA Modules:
  0.0 352.6 jit_solution(14322082575381790667)
XLA Ops:
  0.6 0.0 copy-start
  0.6 3.0 convolution_convert_fusion.1
  3.6 3.5 copy.33
  7.1 0.0 copy-start.3
  7.1 0.0 copy-start.2
  7.1 7.6 %all-to-all-start = ((bf16[32,40,1280]{2,1,0:T(8,128)(2,1)}), bf16[32,40,1280]{2,1,0:T(8,128)(2,1)}, u32[]{:S(2)}, u32[]{:S(2)}) async-start(bf16[32,40,1280]{2,1,0:T(8,128)(2,1)} %copy.33), calls=%async_computation | async-start | bytes 6553600 | tf_op jit(solution)/shard_map/all_to_all | solution.py:21
  14.8 0.0 copy-done.3
  14.8 0.2 reduce-window.8
  15.0 0.0 copy-done.2
  15.0 0.2 fusion.18
  15.2 73.6 %all-to-all-done = bf16[32,40,1280]{2,1,0:T(8,128)(2,1)} async-done(((bf16[32,40,1280]{2,1,0:T(8,128)(2,1)}), bf16[32,40,1280]{2,1,0:T(8,128)(2,1)}, u32[]{:S(2)}, u32[]{:S(2)}) %all-to-all-start) | async-done | bytes 3276832 | tf_op jit(solution)/shard_map/all_to_all | solution.py:21
  88.7 0.0 copy-done
  88.7 23.4 %multiply_reduce_fusion = (f32[]{:T(128)}, f32[1280,1280]{1,0:T(8,128)}) fusion(bf16[1,1280,1280]{2,1,0:T(8,128)(2,1)S(1)} %copy-done, bf16[1280,1280]{1,0:T(8,128)(2,1)} %bitcast.3, bf16[1,1280,1280]{2,1,0:T(8,128)(2,1)} %param.12), kind=kOutput, calls=%fused_computation.9 | convolution fusion | flops 8393523200 | bytes 16384004 | tf_op jit(solution)/shard_map/dot_general | solution.py:34
  112.1 4.2 %multiply_reduce_fusion.1 = f32[]{:T(128)} fusion(bf16[32,40,1280]{2,1,0:T(8,128)(2,1)} %all-to-all-done), kind=kLoop, calls=%fused_computation.10 | loop fusion | flops 4915199 | bytes 3276804 | tf_op jit(solution)/shard_map/reduce_sum | solution.py:44
  116.3 1.3 broadcast_multiply_fusion.1
  117.6 38.1 %all-reduce = (f32[2]{0:T(128)S(1)}, f32[2]{0:T(128)S(1)}) all-reduce(f32[2]{0:T(128)S(1)} %get-tuple-element.21, f32[2]{0:T(128)S(1)} %get-tuple-element.20), channel_id=1, replica_groups=mesh['rep'=1,'fsdp'=32] {'rep','fsdp'}, use_global_device_ids=true, to_apply=%region_5.6 | all-reduce | flops 4 | bytes 32 | tf_op jit(solution)/shard_map/psum | solution.py:46
  155.7 0.6 multiply_reduce_fusion.2
  156.3 4.0 %fusion.5 = bf16[1,1280,1280]{2,1,0:T(8,128)(2,1)S(1)} fusion(f32[1280,1280]{1,0:T(8,128)} %get-tuple-element.23, f32[]{:T(128)} %multiply_reduce_fusion.2), kind=kLoop, calls=%fused_computation.13 | loop fusion | flops 3276800 | bytes 9830404 | tf_op jit(solution)/shard_map/broadcast_in_dim | solution.py:49
  160.3 21.5 %copy.43 = bf16[1,1280,1280]{2,0,1:T(2,128)(2,1)} copy(bf16[1,1280,1280]{2,1,0:T(8,128)(2,1)S(1)} %fusion.5) | data formatting | bytes 6553600 | tf_op jit(solution)/shard_map/broadcast_in_dim | solution.py:49
  181.8 0.5 broadcast.28
  182.3 69.6 %reduce.1 = bf16[1280,1280]{1,0:T(8,128)(2,1)S(1)} reduce(bf16[1280,1,1280]{2,1,0:T(2,128)(2,1)} %bitcast.49, bf16[]{:T(256)} %broadcast.28), dimensions={1}, to_apply=%bitcast.48.reduce_sub_computation | reduce | bytes 6553602
  251.8 2.5 reshape.47
  254.4 5.3 %all-to-all-start.1 = ((bf16[32,2,25600]{2,1,0:T(2,128)(2,1)}), bf16[32,2,25600]{2,1,0:T(2,128)(2,1)S(1)}, u32[]{:S(2)}, u32[]{:S(2)}) async-start(bf16[32,2,25600]{2,1,0:T(2,128)(2,1)} %reshape.47), calls=%async_computation.1 | async-start | bytes 6553600 | tf_op jit(solution)/shard_map/all_to_all | solution.py:49
  259.7 12.2 %fusion.1 = f32[1,1280,1280]{2,1,0:T(8,128)} fusion(bf16[1280,1280]{1,0:T(8,128)(2,1)} %bitcast.3, f32[1,1280,1280]{2,1,0:T(8,128)} %param.10), kind=kOutput, calls=%fused_computation.2 | convolution fusion | flops 4199219200 | bytes 16384000 | tf_op jit(solution)/shard_map/dot_general | solution.py:26
  271.9 12.3 %fusion.4 = f32[1,1280,1280]{2,1,0:T(8,128)} fusion(bf16[32,40,1280]{2,1,0:T(8,128)(2,1)} %all-to-all-done, f32[1,1280,1280]{2,1,0:T(8,128)} %param.11), kind=kOutput, calls=%fused_computation.6 | convolution fusion | flops 4199219200 | bytes 16384000 | tf_op jit(solution)/shard_map/dot_general | solution.py:27
  284.2 49.6 %all-to-all-done.1 = bf16[32,2,25600]{2,1,0:T(2,128)(2,1)S(1)} async-done(((bf16[32,2,25600]{2,1,0:T(2,128)(2,1)}), bf16[32,2,25600]{2,1,0:T(2,128)(2,1)S(1)}, u32[]{:S(2)}, u32[]{:S(2)}) %all-to-all-start.1) | async-done | bytes 3276832 | tf_op jit(solution)/shard_map/all_to_all | solution.py:49
  333.8 12.3 %reshape.48 = bf16[1280,1,1280]{2,1,0:T(2,128)(2,1)} reshape(bf16[32,2,25600]{2,1,0:T(2,128)(2,1)S(1)} %all-to-all-done.1) | data formatting | bytes 6553600
  346.1 3.4 copy.37
  349.4 0.0 copy-start.1
  349.5 0.9 convolution_convert_fusion.2
  350.3 1.9 copy.36
  352.2 0.0 copy-done.1
  (2 shorter events, 0.0 us)
Async XLA Ops:
  0.6 88.1 %copy-start = (bf16[1,1280,1280]{2,1,0:T(8,128)(2,1)S(1)}, bf16[1,1280,1280]{2,1,0:T(8,128)(2,1)}, u32[]{:S(2)}) copy-start(bf16[1,1280,1280]{2,1,0:T(8,128)(2,1)} %param.13) | copy-start | bytes 9830404
  7.1 7.6 %copy-start.3 = (s32[2]{0:T(128)S(1)}, s32[2]{0:T(128)}, u32[]{:S(2)}) copy-start(s32[2]{0:T(128)} %param.8) | copy-start | bytes 28
  7.1 7.8 %copy-start.2 = (s32[24]{0:T(128)S(1)}, s32[24]{0:T(128)}, u32[]{:S(2)}) copy-start(s32[24]{0:T(128)} %param.9) | copy-start | bytes 292
  7.1 81.6 %all-to-all-start = ((bf16[32,40,1280]{2,1,0:T(8,128)(2,1)}), bf16[32,40,1280]{2,1,0:T(8,128)(2,1)}, u32[]{:S(2)}, u32[]{:S(2)}) async-start(bf16[32,40,1280]{2,1,0:T(8,128)(2,1)} %copy.33), calls=%async_computation | async-start | bytes 6553600 | tf_op jit(solution)/shard_map/all_to_all | solution.py:21
  254.4 79.4 %all-to-all-start.1 = ((bf16[32,2,25600]{2,1,0:T(2,128)(2,1)}), bf16[32,2,25600]{2,1,0:T(2,128)(2,1)S(1)}, u32[]{:S(2)}, u32[]{:S(2)}) async-start(bf16[32,2,25600]{2,1,0:T(2,128)(2,1)} %reshape.47), calls=%async_computation.1 | async-start | bytes 6553600 | tf_op jit(solution)/shard_map/all_to_all | solution.py:49
  349.4 2.8 copy-start.1
where the time goes:
time: 356 us; the launch traced here: 353 us
  waiting for transfers between devices  123 us (35%)
  other arithmetic  80 us (22%)
  matrix products  51.7 us (15%)
  local copies, waits for them, and re-layouts  45.6 us (13%)
  blocking collectives  38.1 us (11%)
  starting transfers between devices  12.9 us (4%)
    all_to_all x1, waiting for transfers between devices, on_device(): lax.all_to_all(slotted, 'fsdp', split_axis=0, concat_axis=1, tiled=True)[0]  73.6 us
    unnamed x1, other arithmetic  69.6 us
    all_to_all x1, waiting for transfers between devices, on_device(): lax.all_to_all(scaled[None], 'fsdp', split_axis=1, concat_axis=0, tiled=T...  49.6 us
    psum x1, blocking collectives, on_device(): grad_sq, prec_sq = lax.psum((grad_part, prec_part), ('rep', 'fsdp'))  38.1 us
    dot_general x1, matrix products, on_device(): precond = jnp.dot(halfway, whole_root, preferred_element_type=jnp.float32)  23.4 us
    broadcast_in_dim x1, local copies, waits for them, and re-layouts, on_device(): scaled[None]  21.5 us
    unnamed x13, local copies, waits for them, and re-layouts  20.6 us
    dot_general x1, matrix products, on_device(): lax.dot_general(columns, block, (((0,), (0,)), ((), ())), preferred_eleme...  12.3 us
  transfers between devices with their start and end apart: 2, of which 2 were waited for; matrix products, arithmetic and copies ran while one was open for 7% of the time, Pallas kernels for 0%

commit v1 on v0

v1 whole, which is shorter than its diff:
```python
import jax
import jax.numpy as jnp
from jax import lax
from jax.experimental import pallas as pl
from jax.experimental.pallas import tpu as pltpu
from jax.sharding import PartitionSpec as P

BETA = 0.95
EPSILON = 1e-06
LANES = 128
VMEM = pl.BlockSpec(memory_space=pltpu.VMEM)
SMEM = pl.BlockSpec(memory_space=pltpu.SMEM)
ANY = pl.BlockSpec(memory_space=pl.ANY)


def side(extent, most):
    while extent % most:
        most //= 2
    return most


def pack_kernel(owners, grads, slotted, held, zeros, used, in_sems, out_sems):
    blocks, slots = grads.shape[0], slotted.shape[0]

    def load(b):
        return pltpu.make_async_copy(grads.at[b], held.at[b], in_sems.at[b])

    @pl.loop(0, blocks)
    def _(b):
        load(b).start()

    zeros[...] = jnp.zeros_like(zeros)

    @pl.loop(0, slots)
    def _(s):
        used[s] = 0

    @pl.loop(0, blocks)
    def _(b):
        used[owners[b]] = 1

    @pl.loop(0, slots)
    def _(s):
        @pl.when(used[s] == 0)
        def _():
            pltpu.make_async_copy(zeros, slotted.at[s], out_sems.at[s]).start()

    @pl.loop(0, blocks)
    def _(b):
        load(b).wait()
        s = owners[b]
        pltpu.make_async_copy(held.at[b], slotted.at[s], out_sems.at[s]).start()

    @pl.loop(0, slots)
    def _(s):
        pltpu.make_async_copy(zeros, slotted.at[s], out_sems.at[s]).wait()


def pack(owners, grads, slots):
    blocks, rows, width = grads.shape
    return pl.pallas_call(
        pack_kernel,
        out_shape=jax.ShapeDtypeStruct((slots, rows, width), grads.dtype),
        in_specs=[SMEM, ANY],
        out_specs=ANY,
        scratch_shapes=[
            pltpu.VMEM((blocks, rows, width), grads.dtype),
            pltpu.VMEM((rows, width), grads.dtype),
            pltpu.SMEM((slots,), jnp.int32),
            pltpu.SemaphoreType.DMA((blocks,)),
            pltpu.SemaphoreType.DMA((slots,)),
        ],
        cost_estimate=pl.CostEstimate(flops=0, bytes_accessed=4 * slots * rows * width, transcendentals=0),
        name="pack",
    )(owners, grads)


def unpack_kernel(owners, returned, update, sems):
    blocks = update.shape[0]

    def store(b):
        return pltpu.make_async_copy(returned.at[owners[b]], update.at[b], sems.at[b])

    @pl.loop(0, blocks)
    def _(b):
        store(b).start()

    @pl.loop(0, blocks)
    def _(b):
        store(b).wait()


def unpack(owners, returned):
    blocks = owners.shape[0]
    _, rows, width = returned.shape
    return pl.pallas_call(
        unpack_kernel,
        out_shape=jax.ShapeDtypeStruct((blocks, rows, width), returned.dtype),
        in_specs=[SMEM, VMEM],
        out_specs=ANY,
        scratch_shapes=[pltpu.SemaphoreType.DMA((blocks,))],
        cost_estimate=pl.CostEstimate(flops=0, bytes_accessed=4 * blocks * rows * width, transcendentals=0),
        name="unpack",
    )(owners, returned)


def precond_kernel(left, block, right, grad_part, mine, precond, message, halfway):
    height, width = left.shape
    step = side(width, 256)

    @pl.loop(0, width // step)
    def _(n):
        columns = pl.ds(pl.multiple_of(n * step, step), step)
        part = jnp.dot(left[...], block[:, columns], preferred_element_type=jnp.float32)
        halfway[:, columns] = part.astype(halfway.dtype)

    def body(n, total):
        columns = pl.ds(pl.multiple_of(n * step, step), step)
        part = jnp.dot(halfway[...], right[:, columns], preferred_element_type=jnp.float32)
        precond[:, columns] = part
        squares = jnp.sum((part * part).reshape(height // 8, 8, step), axis=0)
        for k in range(step // LANES):
            total = total + squares[:, k * LANES : (k + 1) * LANES]
        return total

    total = lax.fori_loop(0, width // step, body, jnp.zeros((8, LANES), jnp.float32))
    prec_part = mine[...] * jnp.sum(total, keepdims=True)
    both = jnp.concatenate([grad_part[...], prec_part], axis=0)
    message[...] = jnp.broadcast_to(both[None], message.shape)


def precondition(left, block, right, grad_part, mine, peers):
    height, width = left.shape
    return pl.pallas_call(
        precond_kernel,
        out_shape=(
            jax.ShapeDtypeStruct((height, width), jnp.float32),
            jax.ShapeDtypeStruct((peers, 2, LANES), jnp.float32),
        ),
        in_specs=[VMEM] * 5,
        out_specs=(VMEM, VMEM),
        scratch_shapes=[pltpu.VMEM((height, width), jnp.bfloat16)],
        compiler_params=pltpu.CompilerParams(vmem_limit_bytes=40 << 20),
        cost_estimate=pl.CostEstimate(
            flops=4 * height * width * width, bytes_accessed=12 * width * width, transcendentals=0
        ),
        name="precondition",
    )(left, block, right, grad_part, mine)


def graft_kernel(sums, mine, precond, scaled):
    total = jnp.sum(sums[...], axis=0)
    ratios = jnp.sqrt((total[0:1] + EPSILON) / (total[1:2] + EPSILON))
    ratio = jnp.sum(jnp.where(mine[...] > 0, ratios, 0.0), keepdims=True)
    height = precond.shape[0]
    step = side(height, 128)

    @pl.loop(0, height // step)
    def _(m):
        rows = pl.ds(pl.multiple_of(m * step, step), step)
        scaled[rows, :] = (precond[rows, :] * ratio).astype(scaled.dtype)


def graft(sums, mine, precond):
    return pl.pallas_call(
        graft_kernel,
        out_shape=jax.ShapeDtypeStruct(precond.shape, jnp.bfloat16),
        in_specs=[VMEM] * 3,
        out_specs=VMEM,
        compiler_params=pltpu.CompilerParams(vmem_limit_bytes=40 << 20),
        cost_estimate=pl.CostEstimate(flops=precond.size, bytes_accessed=6 * precond.size, transcendentals=0),
        name="graft",
    )(sums, mine, precond)


def on_device(grads, group_counts, owners, left_stat, right_stat, left_root, right_root):
    slots, reps = lax.axis_size("fsdp"), lax.axis_size("rep")
    width = left_stat.shape[2]
    half_rows = left_stat.shape[1]
    local = grads[0]
    if reps > 1:
        local = lax.psum(local.astype(jnp.float32), "rep").astype(jnp.bfloat16)
    slotted = pack(owners, local, slots)
    block = lax.all_to_all(slotted, "fsdp", split_axis=0, concat_axis=0, tiled=True)
    block = block.reshape(width, width)

    ends = jnp.cumsum(jnp.pad(group_counts, (0, LANES - group_counts.shape[0])))
    starts = ends - jnp.pad(group_counts, (0, LANES - group_counts.shape[0]))
    block_ids = jnp.arange(owners.shape[0], dtype=jnp.int32)
    member = (block_ids[:, None] >= starts[None, :]) & (block_ids[:, None] < ends[None, :])
    owned_here = owners == lax.axis_index("fsdp")
    mine = jnp.sum((member & owned_here[:, None]).astype(jnp.float32), axis=0, keepdims=True)
    local_float = local.astype(jnp.float32)
    squares = jnp.sum(local_float * local_float, axis=(1, 2))
    grad_part = jnp.sum(jnp.where(member, squares[:, None], 0.0), axis=0, keepdims=True)

    whole_root = right_root[0]
    if reps > 1:
        grad_part = grad_part / reps
        whole_root = lax.all_gather(whole_root, "rep", axis=0, tiled=True)
    precond, message = precondition(left_root[0], block, whole_root, grad_part, mine, slots)
    sums = lax.all_to_all(message, "fsdp", split_axis=0, concat_axis=0, tiled=True)
    if reps > 1:
        sums = lax.psum(sums, "rep")
    scaled = graft(sums, mine, precond).reshape(slots, half_rows // slots, width)
    returned = lax.all_to_all(scaled, "fsdp", split_axis=0, concat_axis=0, tiled=True)

    first = lax.axis_index("rep") * half_rows
    rows = lax.dynamic_slice_in_dim(block, first, half_rows, 0) if reps > 1 else block
    columns = lax.dynamic_slice_in_dim(block, first, half_rows, 1) if reps > 1 else block
    coef = (1.0 - BETA) / width
    left_gram = jnp.dot(rows, block.T, preferred_element_type=jnp.float32)
    right_gram = lax.dot_general(columns, block, (((0,), (0,)), ((), ())), preferred_element_type=jnp.float32)
    left_new = BETA * left_stat[0] + coef * left_gram
    right_new = BETA * right_stat[0] + coef * right_gram
    return (left_new[None], right_new[None], unpack(owners, returned))


def solution(mesh):
    in_specs = (
        P("rep", None, "fsdp", None),
        P(),
        P(),
        P("fsdp", "rep", None),
        P("fsdp", "rep", None),
        P("fsdp", "rep", None),
        P("fsdp", "rep", None),
    )
    out_specs = (P("fsdp", "rep", None), P("fsdp", "rep", None), P(None, ("rep", "fsdp"), None))
    return jax.shard_map(on_device, mesh=mesh, in_specs=in_specs, out_specs=out_specs, check_vma=False)
```

time: 356 us -> 202 us (0.57)
  other arithmetic: 80 us -> 2.73 us
  local copies, waits for them, and re-layouts: 45.6 us -> 6.84 us
  matrix products: 51.7 us -> 16.9 us
  blocking collectives: 38.1 us -> 11.1 us
  Pallas kernels: 0 us -> 23.4 us
  waiting for transfers between devices: 123 us -> 129 us
    unnamed x1 -> x0, other arithmetic: 69.6 us -> none
    psum x1 -> x0, blocking collectives: 38.1 us -> none  [on_device(): grad_sq, prec_sq = lax.psum((grad_part, prec_part), ('rep', 'fsdp'))]
    dot_general x4 -> x1, matrix products: 39.4 us -> 8.38 us  [on_device(): left_gram = jnp.dot(rows, block.T, preferred_element_type=jnp.float32)]
    pallas_call x0 -> x4, Pallas kernels: none -> 23.4 us  [the longest x1 13 us: precondition(): pl.pallas_call(precond_kernel, out_shape=(jax.ShapeDtypeStruct((height, w...]
    broadcast_in_dim x1 -> x0, local copies, waits for them, and re-layouts: 21.5 us -> none  [on_device(): scaled[None]]
    unnamed x13 -> x10, local copies, waits for them, and re-layouts: 20.6 us -> 6.72 us
    all_to_all x0 -> x1, blocking collectives: none -> 11.1 us  [on_device(): lax.all_to_all(message, 'fsdp', split_axis=0, concat_axis=0, tiled=True)]
    all_to_all x2, waiting for transfers between devices: 123 us -> 129 us  [the longest x1 71.2 us: on_device(): lax.all_to_all(slotted, 'fsdp', split_axis=0, concat_axis=0, tiled=True)]
  transfers between devices with their start and end apart: 2 -> 2, of which waited for: 2 -> 2; matrix products, arithmetic and copies ran while one was open for 7% -> 10% of each run, Pallas kernels for 0% -> 0%
where the time goes in v1:
time: 202 us; the launch traced here: 201 us
  waiting for transfers between devices  129 us (64%)
  Pallas kernels  23.4 us (12%)
  matrix products  16.9 us (8%)
  blocking collectives  11.1 us (5%)
  starting transfers between devices  10.9 us (5%)
  local copies, waits for them, and re-layouts  6.84 us (3%)
  other arithmetic  2.73 us (1%)
    all_to_all x1, waiting for transfers between devices, on_device(): lax.all_to_all(slotted, 'fsdp', split_axis=0, concat_axis=0, tiled=True)  71.2 us
    all_to_all x1, waiting for transfers between devices, on_device(): lax.all_to_all(scaled, 'fsdp', split_axis=0, concat_axis=0, tiled=True)  57.3 us
    pallas_call x1, Pallas kernels, precondition(): pl.pallas_call(precond_kernel, out_shape=(jax.ShapeDtypeStruct((height, w...  13 us
    all_to_all x1, blocking collectives, on_device(): lax.all_to_all(message, 'fsdp', split_axis=0, concat_axis=0, tiled=True)  11.1 us
    dot_general x1, matrix products, on_device(): lax.dot_general(columns, block, (((0,), (0,)), ((), ())), preferred_eleme...  8.55 us
    dot_general x1, matrix products, on_device(): left_gram = jnp.dot(rows, block.T, preferred_element_type=jnp.float32)  8.38 us
    all_to_all x1, starting transfers between devices, on_device(): lax.all_to_all(slotted, 'fsdp', split_axis=0, concat_axis=0, tiled=True)  7.33 us
    unnamed x10, local copies, waits for them, and re-layouts  6.72 us
  transfers between devices with their start and end apart: 2, of which 2 were waited for; matrix products, arithmetic and copies ran while one was open for 10% of the time, Pallas kernels for 0%

profile of v1, /device:TPU:0, one launch (start us, length us, event | category | flops | bytes accessed | tf_op | source)
XLA Modules:
  0.0 201.1 jit_solution(4152460108162627257)
XLA Ops:
  0.6 0.0 copy-start.4
  0.6 0.0 copy-start.3
  0.7 4.5 %pack.1 = bf16[32,40,1280]{2,1,0:T(8,128)(2,1)} custom-call(s32[24]{0:T(128)} %owners.3, bf16[24,40,1280]{2,1,0:T(8,128)(2,1)} %bitcast.37), custom_call_target="tpu_custom_call" | custom-call | bytes 6553600 | tf_op jit(solution)/shard_map/pack/pallas_call | solution.py:61
  5.2 7.3 %all-to-all-start = ((bf16[32,40,1280]{2,1,0:T(8,128)(2,1)}), bf16[32,40,1280]{2,1,0:T(8,128)(2,1)S(1)}, u32[]{:S(2)}, u32[]{:S(2)}) async-start(bf16[32,40,1280]{2,1,0:T(8,128)(2,1)} %pack.1), calls=%async_computation | async-start | bytes 6553600 | tf_op jit(solution)/shard_map/all_to_all | solution.py:184
  12.5 0.0 copy-done.4
  12.6 0.1 copy.12
  12.7 0.2 reduce-window.8
  12.8 0.1 reduce
  13.0 0.0 copy-done.3
  13.0 2.3 %multiply_reduce_fusion = f32[24]{0:T(128)S(1)} fusion(bf16[1,24,40,1280]{3,2,1,0:T(8,128)(2,1)} %param.7), kind=kLoop, calls=%fused_computation.7 | loop fusion | flops 3686376 | bytes 2457696 | tf_op jit(solution)/shard_map/reduce_sum | solution.py:194
  15.3 0.1 convert_reduce_fusion
  15.4 71.2 %all-to-all-done = bf16[32,40,1280]{2,1,0:T(8,128)(2,1)S(1)} async-done(((bf16[32,40,1280]{2,1,0:T(8,128)(2,1)}), bf16[32,40,1280]{2,1,0:T(8,128)(2,1)S(1)}, u32[]{:S(2)}, u32[]{:S(2)}) %all-to-all-start) | async-done | bytes 3276832 | tf_op jit(solution)/shard_map/all_to_all | solution.py:184
  86.7 0.0 copy-start.1
  86.7 1.9 copy-done.1
  88.6 0.0 copy-start.2
  88.6 1.9 copy-done.2
  90.5 13.0 %precondition.1 = (f32[1280,1280]{1,0:T(8,128)}, f32[32,2,128]{2,1,0:T(2,128)S(1)}) custom-call(bf16[1280,1280]{1,0:T(8,128)(2,1)S(1)} %bitcast.35, bf16[1280,1280]{1,0:T(8,128)(2,1)S(1)} %bitcast.30, bf16[1280,1280]{1,0:T(8,128)(2,1)S(1)} %bitcast.36, f32[1,128]{1,0:T(1,128)S(1)} %bitcast.34, f32[1,128]{1,0:T(1,128)S(1)} %bitcast.32), custom_call_target="tpu_custom_call" | custom-call | flops 8388608000 | bytes 19660800 | tf_op jit(solution)/shard_map/precondition/pallas_call | solution.py:134
  103.5 11.1 %all_to_all.15.sums = f32[32,2,128]{2,1,0:T(2,128)S(1)} all-to-all(f32[32,2,128]{2,1,0:T(2,128)S(1)} %get-tuple-element.5), channel_id=1, replica_groups=mesh['rep'=1,'fsdp'=32] {'fsdp'}, dimensions={0} | all-to-all | bytes 65536 | tf_op jit(solution)/shard_map/all_to_all | solution.py:202
  114.6 0.0 copy-start
  114.6 2.9 %copy-done = f32[1280,1280]{1,0:T(8,128)S(1)} copy-done((f32[1280,1280]{1,0:T(8,128)S(1)}, f32[1280,1280]{1,0:T(8,128)}, u32[]{:S(2)}) %copy-start) | copy-done | bytes 6553624
  117.5 2.3 %graft.1 = bf16[1280,1280]{1,0:T(8,128)(2,1)} custom-call(f32[32,2,128]{2,1,0:T(2,128)S(1)} %all_to_all.15.sums, f32[1,128]{1,0:T(1,128)S(1)} %bitcast.33, f32[1280,1280]{1,0:T(8,128)S(1)} %copy-done), custom_call_target="tpu_custom_call" | custom-call | flops 1638400 | bytes 9830400 | tf_op jit(solution)/shard_map/graft/pallas_call | solution.py:165
  119.8 3.5 %all-to-all-start.2 = ((bf16[32,40,1280]{2,1,0:T(8,128)(2,1)}), bf16[32,40,1280]{2,1,0:T(8,128)(2,1)}, u32[]{:S(2)}, u32[]{:S(2)}) async-start(bf16[32,40,1280]{2,1,0:T(8,128)(2,1)} %bitcast.12), calls=%async_computation.2 | async-start | bytes 6553600 | tf_op jit(solution)/shard_map/all_to_all | solution.py:206
  123.3 8.4 %fusion.1 = f32[1,1280,1280]{2,1,0:T(8,128)} fusion(bf16[1280,1280]{1,0:T(8,128)(2,1)S(1)} %bitcast.31, f32[1,1280,1280]{2,1,0:T(8,128)} %param.10), kind=kOutput, calls=%fused_computation.2 | convolution fusion | flops 4199219200 | bytes 16384000 | tf_op jit(solution)/shard_map/dot_general | solution.py:212
  131.7 8.6 %fusion.4 = f32[1,1280,1280]{2,1,0:T(8,128)} fusion(bf16[32,40,1280]{2,1,0:T(8,128)(2,1)S(1)} %all-to-all-done, f32[1,1280,1280]{2,1,0:T(8,128)} %param.11), kind=kOutput, calls=%fused_computation.6 | convolution fusion | flops 4199219200 | bytes 16384000 | tf_op jit(solution)/shard_map/dot_general | solution.py:213
  140.2 57.3 %all-to-all-done.2.returned = bf16[32,40,1280]{2,1,0:T(8,128)(2,1)} async-done(((bf16[32,40,1280]{2,1,0:T(8,128)(2,1)}), bf16[32,40,1280]{2,1,0:T(8,128)(2,1)}, u32[]{:S(2)}, u32[]{:S(2)}) %all-to-all-start.2) | async-done | bytes 3276832 | tf_op jit(solution)/shard_map/all_to_all | solution.py:206
  197.5 3.6 %unpack.1 = bf16[24,40,1280]{2,1,0:T(8,128)(2,1)} custom-call(s32[24]{0:T(128)} %owners.3, bf16[32,40,1280]{2,1,0:T(8,128)(2,1)} %all-to-all-done.2.returned), custom_call_target="tpu_custom_call" | custom-call | bytes 4915200 | tf_op jit(solution)/shard_map/unpack/pallas_call | solution.py:96
  (3 shorter events, 0.0 us)
Async XLA Ops:
  0.6 11.9 %copy-start.4 = (s32[2]{0:T(128)S(1)}, s32[2]{0:T(128)}, u32[]{:S(2)}) copy-start(s32[2]{0:T(128)} %param.8) | copy-start | bytes 28
  0.6 12.3 %copy-start.3 = (s32[24]{0:T(128)S(1)}, s32[24]{0:T(128)}, u32[]{:S(2)}) copy-start(s32[24]{0:T(128)} %owners.3) | copy-start | bytes 292
  5.2 81.5 %all-to-all-start = ((bf16[32,40,1280]{2,1,0:T(8,128)(2,1)}), bf16[32,40,1280]{2,1,0:T(8,128)(2,1)S(1)}, u32[]{:S(2)}, u32[]{:S(2)}) async-start(bf16[32,40,1280]{2,1,0:T(8,128)(2,1)} %pack.1), calls=%async_computation | async-start | bytes 6553600 | tf_op jit(solution)/shard_map/all_to_all | solution.py:184
  86.7 1.9 copy-start.1
  88.6 1.9 copy-start.2
  114.6 2.9 %copy-start = (f32[1280,1280]{1,0:T(8,128)S(1)}, f32[1280,1280]{1,0:T(8,128)}, u32[]{:S(2)}) copy-start(f32[1280,1280]{1,0:T(8,128)} %get-tuple-element.6.precond) | copy-start | bytes 19660804
  119.8 77.8 %all-to-all-start.2 = ((bf16[32,40,1280]{2,1,0:T(8,128)(2,1)}), bf16[32,40,1280]{2,1,0:T(8,128)(2,1)}, u32[]{:S(2)}, u32[]{:S(2)}) async-start(bf16[32,40,1280]{2,1,0:T(8,128)(2,1)} %bitcast.12), calls=%async_computation.2 | async-start | bytes 6553600 | tf_op jit(solution)/shard_map/all_to_all | solution.py:206

commit v2 on v1

--- a/solution.py
+++ b/solution.py
@@ -8,9 +8,10 @@
 BETA = 0.95
 EPSILON = 1e-06
 LANES = 128
+KERNEL_VMEM = 32 << 20
 VMEM = pl.BlockSpec(memory_space=pltpu.VMEM)
 SMEM = pl.BlockSpec(memory_space=pltpu.SMEM)
-ANY = pl.BlockSpec(memory_space=pl.ANY)
+HBM = pl.BlockSpec(memory_space=pltpu.HBM)
 
 
 def side(extent, most):
@@ -21,38 +22,25 @@
 
 def pack_kernel(owners, grads, slotted, held, zeros, used, in_sems, out_sems):
     blocks, slots = grads.shape[0], slotted.shape[0]
-
-    def load(b):
-        return pltpu.make_async_copy(grads.at[b], held.at[b], in_sems.at[b])
-
-    @pl.loop(0, blocks)
-    def _(b):
-        load(b).start()
-
+    loads = [pltpu.make_async_copy(grads.at[b], held.at[b], in_sems.at[b]) for b in range(blocks)]
+    for load in loads:
+        load.start()
     zeros[...] = jnp.zeros_like(zeros)
-
-    @pl.loop(0, slots)
-    def _(s):
+    for s in range(slots):
         used[s] = 0
-
-    @pl.loop(0, blocks)
-    def _(b):
+    for b in range(blocks):
         used[owners[b]] = 1
-
-    @pl.loop(0, slots)
-    def _(s):
+    for s in range(slots):
+
         @pl.when(used[s] == 0)
         def _():
             pltpu.make_async_copy(zeros, slotted.at[s], out_sems.at[s]).start()
 
-    @pl.loop(0, blocks)
-    def _(b):
-        load(b).wait()
+    for b in range(blocks):
+        loads[b].wait()
         s = owners[b]
         pltpu.make_async_copy(held.at[b], slotted.at[s], out_sems.at[s]).start()
-
-    @pl.loop(0, slots)
-    def _(s):
+    for s in range(slots):
         pltpu.make_async_copy(zeros, slotted.at[s], out_sems.at[s]).wait()
 
 
@@ -61,8 +49,8 @@
     return pl.pallas_call(
         pack_kernel,
         out_shape=jax.ShapeDtypeStruct((slots, rows, width), grads.dtype),
-        in_specs=[SMEM, ANY],
-        out_specs=ANY,
+        in_specs=[SMEM, HBM],
+        out_specs=HBM,
         scratch_shapes=[
             pltpu.VMEM((blocks, rows, width), grads.dtype),
             pltpu.VMEM((rows, width), grads.dtype),
@@ -75,19 +63,17 @@
     )(owners, grads)
 
 
-def unpack_kernel(owners, returned, update, sems):
+def unpack_kernel(owners, returned, update, held, in_sems, out_sems):
     blocks = update.shape[0]
-
-    def store(b):
-        return pltpu.make_async_copy(returned.at[owners[b]], update.at[b], sems.at[b])
-
-    @pl.loop(0, blocks)
-    def _(b):
-        store(b).start()
-
-    @pl.loop(0, blocks)
-    def _(b):
-        store(b).wait()
+    loads = [pltpu.make_async_copy(returned.at[owners[b]], held.at[b], in_sems.at[b]) for b in range(blocks)]
+    stores = [pltpu.make_async_copy(held.at[b], update.at[b], out_sems.at[b]) for b in range(blocks)]
+    for load in loads:
+        load.start()
+    for load, store in zip(loads, stores):
+        load.wait()
+        store.start()
+    for store in stores:
+        store.wait()
 
 
 def unpack(owners, returned):
@@ -96,34 +82,42 @@
     return pl.pallas_call(
         unpack_kernel,
         out_shape=jax.ShapeDtypeStruct((blocks, rows, width), returned.dtype),
-        in_specs=[SMEM, VMEM],
-        out_specs=ANY,
-        scratch_shapes=[pltpu.SemaphoreType.DMA((blocks,))],
+        in_specs=[SMEM, HBM],
+        out_specs=HBM,
+        scratch_shapes=[
+            pltpu.VMEM((blocks, rows, width), returned.dtype),
+            pltpu.SemaphoreType.DMA((blocks,)),
+            pltpu.SemaphoreType.DMA((blocks,)),
+        ],
         cost_estimate=pl.CostEstimate(flops=0, bytes_accessed=4 * blocks * rows * width, transcendentals=0),
         name="unpack",
     )(owners, returned)
 
 
-def precond_kernel(left, block, right, grad_part, mine, precond, message, halfway):
+def precond_kernel(left, block, right, grad_part, mine, precond, message, left_held, right_held, halfway, sems):
     height, width = left.shape
-    step = side(width, 256)
-
-    @pl.loop(0, width // step)
-    def _(n):
-        columns = pl.ds(pl.multiple_of(n * step, step), step)
-        part = jnp.dot(left[...], block[:, columns], preferred_element_type=jnp.float32)
-        halfway[:, columns] = part.astype(halfway.dtype)
-
-    def body(n, total):
-        columns = pl.ds(pl.multiple_of(n * step, step), step)
-        part = jnp.dot(halfway[...], right[:, columns], preferred_element_type=jnp.float32)
-        precond[:, columns] = part
-        squares = jnp.sum((part * part).reshape(height // 8, 8, step), axis=0)
-        for k in range(step // LANES):
-            total = total + squares[:, k * LANES : (k + 1) * LANES]
-        return total
-
-    total = lax.fori_loop(0, width // step, body, jnp.zeros((8, LANES), jnp.float32))
+    lead, tile = side(height, 256), side(width, 256)
+    spans = [pl.ds(0, lead), pl.ds(lead, height - lead)]
+    tiles = [pl.ds(k * tile, tile) for k in range(width // tile)]
+    loads = [pltpu.make_async_copy(left.at[r], left_held.at[r], sems.at[0, m]) for m, r in enumerate(spans)]
+    rights = [pltpu.make_async_copy(right.at[k], right_held.at[k], sems.at[1, i]) for i, k in enumerate(tiles)]
+    for copy in loads[:1] + rights + loads[1:]:
+        copy.start()
+    total = jnp.zeros((8, LANES), jnp.float32)
+    for m, rows in enumerate(spans):
+        loads[m].wait()
+        for n in tiles:
+            part = jnp.dot(left_held[rows, :], block[:, n], preferred_element_type=jnp.float32)
+            halfway[rows, n] = part.astype(halfway.dtype)
+        if m == 0:
+            for copy in rights:
+                copy.wait()
+        for n in tiles:
+            part = jnp.dot(halfway[rows, :], right_held[:, n], preferred_element_type=jnp.float32)
+            precond[rows, n] = part
+            squares = jnp.sum((part * part).reshape(rows.size // 8, 8, tile), axis=0)
+            for k in range(tile // LANES):
+                total = total + squares[:, k * LANES : (k + 1) * LANES]
     prec_part = mine[...] * jnp.sum(total, keepdims=True)
     both = jnp.concatenate([grad_part[...], prec_part], axis=0)
     message[...] = jnp.broadcast_to(both[None], message.shape)
@@ -131,16 +125,20 @@
 
 def precondition(left, block, right, grad_part, mine, peers):
     height, width = left.shape
+    left = pltpu.with_memory_space_constraint(left, pltpu.HBM)
+    right = pltpu.with_memory_space_constraint(right, pltpu.HBM)
     return pl.pallas_call(
         precond_kernel,
-        out_shape=(
-            jax.ShapeDtypeStruct((height, width), jnp.float32),
-            jax.ShapeDtypeStruct((peers, 2, LANES), jnp.float32),
-        ),
-        in_specs=[VMEM] * 5,
+        out_shape=(pltpu.VMEM((height, width), jnp.float32), pltpu.VMEM((peers, 2, LANES), jnp.float32)),
+        in_specs=[HBM, VMEM, HBM, VMEM, VMEM],
         out_specs=(VMEM, VMEM),
-        scratch_shapes=[pltpu.VMEM((height, width), jnp.bfloat16)],
-        compiler_params=pltpu.CompilerParams(vmem_limit_bytes=40 << 20),
+        scratch_shapes=[
+            pltpu.VMEM((height, width), jnp.bfloat16),
+            pltpu.VMEM((width, width), jnp.bfloat16),
+            pltpu.VMEM((height, width), jnp.bfloat16),
+            pltpu.SemaphoreType.DMA((2, max(2, width // side(width, 256)))),
+        ],
+        compiler_params=pltpu.CompilerParams(vmem_limit_bytes=KERNEL_VMEM),
         cost_estimate=pl.CostEstimate(
             flops=4 * height * width * width, bytes_accessed=12 * width * width, transcendentals=0
         ),
@@ -165,9 +163,9 @@
     return pl.pallas_call(
         graft_kernel,
         out_shape=jax.ShapeDtypeStruct(precond.shape, jnp.bfloat16),
-        in_specs=[VMEM] * 3,
+        in_specs=[VMEM, VMEM, VMEM],
         out_specs=VMEM,
-        compiler_params=pltpu.CompilerParams(vmem_limit_bytes=40 << 20),
+        compiler_params=pltpu.CompilerParams(vmem_limit_bytes=KERNEL_VMEM),
         cost_estimate=pl.CostEstimate(flops=precond.size, bytes_accessed=6 * precond.size, transcendentals=0),
         name="graft",
     )(sums, mine, precond)

time: 202 us -> 192 us (0.950)
  local copies, waits for them, and re-layouts: 6.84 us -> 0.13 us
  Pallas kernels: 23.4 us -> 20.6 us
    unnamed x10 -> x4, local copies, waits for them, and re-layouts: 6.72 us -> 0.01 us
    pallas_call x1, Pallas kernels: 13 us -> 10.7 us  [precondition(): pl.pallas_call(precond_kernel, out_shape=(pltpu.VMEM((height, width), jnp...]
where the time goes in v2:
time: 192 us
  waiting for transfers between devices  128 us (67%)
  Pallas kernels  20.6 us (11%)
  matrix products  16.9 us (9%)
  starting transfers between devices  11.1 us (6%)
  blocking collectives  11.1 us (6%)
  other arithmetic  2.73 us (1%)
    all_to_all x1, waiting for transfers between devices, on_device(): lax.all_to_all(slotted, 'fsdp', split_axis=0, concat_axis=0, tiled=True)  71.2 us
    all_to_all x1, waiting for transfers between devices, on_device(): lax.all_to_all(scaled, 'fsdp', split_axis=0, concat_axis=0, tiled=True)  57.2 us
    all_to_all x1, blocking collectives, on_device(): lax.all_to_all(message, 'fsdp', split_axis=0, concat_axis=0, tiled=True)  11.1 us
    pallas_call x1, Pallas kernels, precondition(): pl.pallas_call(precond_kernel, out_shape=(pltpu.VMEM((height, width), jnp...  10.7 us
    dot_general x1, matrix products, on_device(): lax.dot_general(columns, block, (((0,), (0,)), ((), ())), preferred_eleme...  8.55 us
    dot_general x1, matrix products, on_device(): left_gram = jnp.dot(rows, block.T, preferred_element_type=jnp.float32)  8.39 us
    all_to_all x1, starting transfers between devices, on_device(): lax.all_to_all(slotted, 'fsdp', split_axis=0, concat_axis=0, tiled=True)  7.33 us
    pallas_call x1, Pallas kernels, pack(): pl.pallas_call(pack_kernel, out_shape=jax.ShapeDtypeStruct((slots, rows,...  4.06 us
  transfers between devices with their start and end apart: 2, of which 2 were waited for; matrix products, arithmetic and copies ran while one was open for 10% of the time, Pallas kernels for 0%

profile of v2, /device:TPU:0, one launch (start us, length us, event | category | flops | bytes accessed | tf_op | source)
XLA Modules:
  0.0 191.8 jit_solution(5314574870231114732)
XLA Ops:
  0.6 0.0 copy-start.1
  0.6 0.0 copy-start
  0.7 4.1 %pack.1 = bf16[32,40,1280]{2,1,0:T(8,128)(2,1)} custom-call(s32[24]{0:T(128)} %owners.3, bf16[24,40,1280]{2,1,0:T(8,128)(2,1)} %bitcast.35), custom_call_target="tpu_custom_call" | custom-call | bytes 6553600 | tf_op jit(solution)/shard_map/pack/pallas_call | solution.py:49
  4.7 7.3 %all-to-all-start = ((bf16[32,40,1280]{2,1,0:T(8,128)(2,1)}), bf16[32,40,1280]{2,1,0:T(8,128)(2,1)S(1)}, u32[]{:S(2)}, u32[]{:S(2)}) async-start(bf16[32,40,1280]{2,1,0:T(8,128)(2,1)} %pack.1), calls=%async_computation | async-start | bytes 6553600 | tf_op jit(solution)/shard_map/all_to_all | solution.py:182
  12.1 0.0 copy-done.1
  12.1 0.1 copy.12
  12.2 0.2 reduce-window.8
  12.4 0.1 reduce
  12.5 0.0 copy-done
  12.5 2.3 %multiply_reduce_fusion = f32[24]{0:T(128)S(1)} fusion(bf16[1,24,40,1280]{3,2,1,0:T(8,128)(2,1)} %param.7), kind=kLoop, calls=%fused_computation.7 | loop fusion | flops 3686376 | bytes 2457696 | tf_op jit(solution)/shard_map/reduce_sum | solution.py:192
  14.9 0.1 convert_reduce_fusion
  15.0 71.2 %all-to-all-done = bf16[32,40,1280]{2,1,0:T(8,128)(2,1)S(1)} async-done(((bf16[32,40,1280]{2,1,0:T(8,128)(2,1)}), bf16[32,40,1280]{2,1,0:T(8,128)(2,1)S(1)}, u32[]{:S(2)}, u32[]{:S(2)}) %all-to-all-start) | async-done | bytes 3276832 | tf_op jit(solution)/shard_map/all_to_all | solution.py:182
  86.2 10.7 %precondition.1 = (f32[1280,1280]{1,0:T(8,128)S(1)}, f32[32,2,128]{2,1,0:T(2,128)S(1)}) custom-call(bf16[1280,1280]{1,0:T(8,128)(2,1)} %bitcast.36, bf16[1280,1280]{1,0:T(8,128)(2,1)S(1)} %bitcast.30, bf16[1280,1280]{1,0:T(8,128)(2,1)} %bitcast.37, f32[1,128]{1,0:T(1,128)S(1)} %bitcast.34, f32[1,128]{1,0:T(1,128)S(1)} %bitcast.32), custom_call_target="tpu_custom_call" | custom-call | flops 8388608000 | bytes 19660800 | tf_op jit(solution)/shard_map/precondition/pallas_call | solution.py:130
  96.9 11.1 %all_to_all.15.sums = f32[32,2,128]{2,1,0:T(2,128)S(1)} all-to-all(f32[32,2,128]{2,1,0:T(2,128)S(1)} %get-tuple-element.5), channel_id=1, replica_groups=mesh['rep'=1,'fsdp'=32] {'fsdp'}, dimensions={0} | all-to-all | bytes 65536 | tf_op jit(solution)/shard_map/all_to_all | solution.py:200
  108.0 2.3 %graft.1 = bf16[1280,1280]{1,0:T(8,128)(2,1)} custom-call(f32[32,2,128]{2,1,0:T(2,128)S(1)} %all_to_all.15.sums, f32[1,128]{1,0:T(1,128)S(1)} %bitcast.33, f32[1280,1280]{1,0:T(8,128)S(1)} %get-tuple-element.6.precond), custom_call_target="tpu_custom_call" | custom-call | flops 1638400 | bytes 9830400 | tf_op jit(solution)/shard_map/graft/pallas_call | solution.py:163
  110.3 3.7 %all-to-all-start.2 = ((bf16[32,40,1280]{2,1,0:T(8,128)(2,1)}), bf16[32,40,1280]{2,1,0:T(8,128)(2,1)}, u32[]{:S(2)}, u32[]{:S(2)}) async-start(bf16[32,40,1280]{2,1,0:T(8,128)(2,1)} %bitcast.12), calls=%async_computation.2 | async-start | bytes 6553600 | tf_op jit(solution)/shard_map/all_to_all | solution.py:204
  114.0 8.4 %fusion.1 = f32[1,1280,1280]{2,1,0:T(8,128)} fusion(bf16[1280,1280]{1,0:T(8,128)(2,1)S(1)} %bitcast.31, f32[1,1280,1280]{2,1,0:T(8,128)} %param.10), kind=kOutput, calls=%fused_computation.2 | convolution fusion | flops 4199219200 | bytes 16384000 | tf_op jit(solution)/shard_map/dot_general | solution.py:210
  122.4 8.6 %fusion.4 = f32[1,1280,1280]{2,1,0:T(8,128)} fusion(bf16[32,40,1280]{2,1,0:T(8,128)(2,1)S(1)} %all-to-all-done, f32[1,1280,1280]{2,1,0:T(8,128)} %param.11), kind=kOutput, calls=%fused_computation.6 | convolution fusion | flops 4199219200 | bytes 16384000 | tf_op jit(solution)/shard_map/dot_general | solution.py:211
  131.0 57.2 %all-to-all-done.2.returned = bf16[32,40,1280]{2,1,0:T(8,128)(2,1)} async-done(((bf16[32,40,1280]{2,1,0:T(8,128)(2,1)}), bf16[32,40,1280]{2,1,0:T(8,128)(2,1)}, u32[]{:S(2)}, u32[]{:S(2)}) %all-to-all-start.2) | async-done | bytes 3276832 | tf_op jit(solution)/shard_map/all_to_all | solution.py:204
  188.2 3.5 %unpack.1 = bf16[24,40,1280]{2,1,0:T(8,128)(2,1)} custom-call(s32[24]{0:T(128)} %owners.3, bf16[32,40,1280]{2,1,0:T(8,128)(2,1)} %all-to-all-done.2.returned), custom_call_target="tpu_custom_call" | custom-call | bytes 4915200 | tf_op jit(solution)/shard_map/unpack/pallas_call | solution.py:82
  (3 shorter events, 0.0 us)
Async XLA Ops:
  0.6 11.4 %copy-start.1 = (s32[2]{0:T(128)S(1)}, s32[2]{0:T(128)}, u32[]{:S(2)}) copy-start(s32[2]{0:T(128)} %param.8) | copy-start | bytes 28
  0.6 11.8 %copy-start = (s32[24]{0:T(128)S(1)}, s32[24]{0:T(128)}, u32[]{:S(2)}) copy-start(s32[24]{0:T(128)} %owners.3) | copy-start | bytes 292
  4.7 81.5 %all-to-all-start = ((bf16[32,40,1280]{2,1,0:T(8,128)(2,1)}), bf16[32,40,1280]{2,1,0:T(8,128)(2,1)S(1)}, u32[]{:S(2)}, u32[]{:S(2)}) async-start(bf16[32,40,1280]{2,1,0:T(8,128)(2,1)} %pack.1), calls=%async_computation | async-start | bytes 6553600 | tf_op jit(solution)/shard_map/all_to_all | solution.py:182
  110.3 77.9 %all-to-all-start.2 = ((bf16[32,40,1280]{2,1,0:T(8,128)(2,1)}), bf16[32,40,1280]{2,1,0:T(8,128)(2,1)}, u32[]{:S(2)}, u32[]{:S(2)}) async-start(bf16[32,40,1280]{2,1,0:T(8,128)(2,1)} %bitcast.12), calls=%async_computation.2 | async-start | bytes 6553600 | tf_op jit(solution)/shard_map/all_to_all | solution.py:204

commit v3 on v2

--- a/solution.py
+++ b/solution.py
@@ -20,14 +20,17 @@
     return most
 
 
-def pack_kernel(owners, grads, slotted, held, zeros, used, in_sems, out_sems):
+def pack_kernel(owners_far, grads, slotted, held, zeros, owners, used, owner_sem, in_sems, out_sems):
     blocks, slots = grads.shape[0], slotted.shape[0]
     loads = [pltpu.make_async_copy(grads.at[b], held.at[b], in_sems.at[b]) for b in range(blocks)]
+    load_owners = pltpu.make_async_copy(owners_far, owners, owner_sem)
+    load_owners.start()
     for load in loads:
         load.start()
     zeros[...] = jnp.zeros_like(zeros)
     for s in range(slots):
         used[s] = 0
+    load_owners.wait()
     for b in range(blocks):
         used[owners[b]] = 1
     for s in range(slots):
@@ -49,28 +52,26 @@
     return pl.pallas_call(
         pack_kernel,
         out_shape=jax.ShapeDtypeStruct((slots, rows, width), grads.dtype),
-        in_specs=[SMEM, HBM],
+        in_specs=[HBM, HBM],
         out_specs=HBM,
         scratch_shapes=[
             pltpu.VMEM((blocks, rows, width), grads.dtype),
             pltpu.VMEM((rows, width), grads.dtype),
+            pltpu.SMEM((blocks,), jnp.int32),
             pltpu.SMEM((slots,), jnp.int32),
+            pltpu.SemaphoreType.DMA,
             pltpu.SemaphoreType.DMA((blocks,)),
             pltpu.SemaphoreType.DMA((slots,)),
         ],
         cost_estimate=pl.CostEstimate(flops=0, bytes_accessed=4 * slots * rows * width, transcendentals=0),
         name="pack",
-    )(owners, grads)
-
-
-def unpack_kernel(owners, returned, update, held, in_sems, out_sems):
+    )(pltpu.with_memory_space_constraint(owners, pltpu.HBM), grads)
+
+
+def unpack_kernel(owners, returned, update, sems):
     blocks = update.shape[0]
-    loads = [pltpu.make_async_copy(returned.at[owners[b]], held.at[b], in_sems.at[b]) for b in range(blocks)]
-    stores = [pltpu.make_async_copy(held.at[b], update.at[b], out_sems.at[b]) for b in range(blocks)]
-    for load in loads:
-        load.start()
-    for load, store in zip(loads, stores):
-        load.wait()
+    stores = [pltpu.make_async_copy(returned.at[owners[b]], update.at[b], sems.at[b]) for b in range(blocks)]
+    for store in stores:
         store.start()
     for store in stores:
         store.wait()
@@ -82,25 +83,25 @@
     return pl.pallas_call(
         unpack_kernel,
         out_shape=jax.ShapeDtypeStruct((blocks, rows, width), returned.dtype),
-        in_specs=[SMEM, HBM],
+        in_specs=[SMEM, VMEM],
         out_specs=HBM,
-        scratch_shapes=[
-            pltpu.VMEM((blocks, rows, width), returned.dtype),
-            pltpu.SemaphoreType.DMA((blocks,)),
-            pltpu.SemaphoreType.DMA((blocks,)),
-        ],
+        scratch_shapes=[pltpu.SemaphoreType.DMA((blocks,))],
+        compiler_params=pltpu.CompilerParams(vmem_limit_bytes=KERNEL_VMEM),
         cost_estimate=pl.CostEstimate(flops=0, bytes_accessed=4 * blocks * rows * width, transcendentals=0),
         name="unpack",
     )(owners, returned)
 
 
-def precond_kernel(left, block, right, grad_part, mine, precond, message, left_held, right_held, halfway, sems):
+def precond_kernel(
+    left, block, right, grad_part, mine, precond, message, kept, left_held, right_held, halfway, sems
+):
     height, width = left.shape
     lead, tile = side(height, 256), side(width, 256)
     spans = [pl.ds(0, lead), pl.ds(lead, height - lead)]
     tiles = [pl.ds(k * tile, tile) for k in range(width // tile)]
     loads = [pltpu.make_async_copy(left.at[r], left_held.at[r], sems.at[0, m]) for m, r in enumerate(spans)]
     rights = [pltpu.make_async_copy(right.at[k], right_held.at[k], sems.at[1, i]) for i, k in enumerate(tiles)]
+    keep = pltpu.make_async_copy(block, kept, sems.at[0, len(spans)])
     for copy in loads[:1] + rights + loads[1:]:
         copy.start()
     total = jnp.zeros((8, LANES), jnp.float32)
@@ -112,6 +113,7 @@
         if m == 0:
             for copy in rights:
                 copy.wait()
+            keep.start()
         for n in tiles:
             part = jnp.dot(halfway[rows, :], right_held[:, n], preferred_element_type=jnp.float32)
             precond[rows, n] = part
@@ -121,6 +123,7 @@
     prec_part = mine[...] * jnp.sum(total, keepdims=True)
     both = jnp.concatenate([grad_part[...], prec_part], axis=0)
     message[...] = jnp.broadcast_to(both[None], message.shape)
+    keep.wait()
 
 
 def precondition(left, block, right, grad_part, mine, peers):
@@ -129,14 +132,18 @@
     right = pltpu.with_memory_space_constraint(right, pltpu.HBM)
     return pl.pallas_call(
         precond_kernel,
-        out_shape=(pltpu.VMEM((height, width), jnp.float32), pltpu.VMEM((peers, 2, LANES), jnp.float32)),
+        out_shape=(
+            pltpu.VMEM((height, width), jnp.float32),
+            pltpu.VMEM((peers, 2, LANES), jnp.float32),
+            pltpu.HBM(block.shape, block.dtype),
+        ),
         in_specs=[HBM, VMEM, HBM, VMEM, VMEM],
-        out_specs=(VMEM, VMEM),
+        out_specs=(VMEM, VMEM, HBM),
         scratch_shapes=[
             pltpu.VMEM((height, width), jnp.bfloat16),
             pltpu.VMEM((width, width), jnp.bfloat16),
             pltpu.VMEM((height, width), jnp.bfloat16),
-            pltpu.SemaphoreType.DMA((2, max(2, width // side(width, 256)))),
+            pltpu.SemaphoreType.DMA((2, max(3, width // side(width, 256)))),
         ],
         compiler_params=pltpu.CompilerParams(vmem_limit_bytes=KERNEL_VMEM),
         cost_estimate=pl.CostEstimate(
@@ -146,25 +153,32 @@
     )(left, block, right, grad_part, mine)
 
 
-def graft_kernel(sums, mine, precond, scaled):
+def graft_kernel(sums, mine, precond, scaled, out, sems):
     total = jnp.sum(sums[...], axis=0)
     ratios = jnp.sqrt((total[0:1] + EPSILON) / (total[1:2] + EPSILON))
     ratio = jnp.sum(jnp.where(mine[...] > 0, ratios, 0.0), keepdims=True)
     height = precond.shape[0]
     step = side(height, 128)
-
-    @pl.loop(0, height // step)
-    def _(m):
-        rows = pl.ds(pl.multiple_of(m * step, step), step)
-        scaled[rows, :] = (precond[rows, :] * ratio).astype(scaled.dtype)
+    spans = [pl.ds(m, step) for m in range(0, height, step)]
+    stores = [pltpu.make_async_copy(out.at[r], scaled.at[r], sems.at[i]) for i, r in enumerate(spans)]
+    for rows, store in zip(spans, stores):
+        out[rows, :] = (precond[rows, :] * ratio).astype(out.dtype)
+        store.start()
+    for store in stores:
+        store.wait()
 
 
 def graft(sums, mine, precond):
+    height = precond.shape[0]
     return pl.pallas_call(
         graft_kernel,
-        out_shape=jax.ShapeDtypeStruct(precond.shape, jnp.bfloat16),
+        out_shape=pltpu.HBM(precond.shape, jnp.bfloat16),
         in_specs=[VMEM, VMEM, VMEM],
-        out_specs=VMEM,
+        out_specs=HBM,
+        scratch_shapes=[
+            pltpu.VMEM(precond.shape, jnp.bfloat16),
+            pltpu.SemaphoreType.DMA((height // side(height, 128),)),
+        ],
         compiler_params=pltpu.CompilerParams(vmem_limit_bytes=KERNEL_VMEM),
         cost_estimate=pl.CostEstimate(flops=precond.size, bytes_accessed=6 * precond.size, transcendentals=0),
         name="graft",
@@ -196,7 +210,7 @@
     if reps > 1:
         grad_part = grad_part / reps
         whole_root = lax.all_gather(whole_root, "rep", axis=0, tiled=True)
-    precond, message = precondition(left_root[0], block, whole_root, grad_part, mine, slots)
+    precond, message, block = precondition(left_root[0], block, whole_root, grad_part, mine, slots)
     sums = lax.all_to_all(message, "fsdp", split_axis=0, concat_axis=0, tiled=True)
     if reps > 1:
         sums = lax.psum(sums, "rep")

time: 192 us -> 189 us (0.984)
  matrix products: 16.9 us -> 20.9 us
  waiting for transfers between devices: 128 us -> 124 us
  Pallas kernels: 20.6 us -> 18 us
    all_to_all x1, waiting for transfers between devices: 57.2 us -> 53.2 us  [on_device(): lax.all_to_all(scaled, 'fsdp', split_axis=0, concat_axis=0, tiled=True)]
    dot_general x1, matrix products: 8.55 us -> 12.4 us  [on_device(): lax.dot_general(columns, block, (((0,), (0,)), ((), ())), preferred_eleme...]
  transfers between devices with their start and end apart: 2 -> 2, of which waited for: 2 -> 2; matrix products, arithmetic and copies ran while one was open for 10% -> 13% of each run, Pallas kernels for 0% -> 0%
where the time goes in v3:
time: 189 us
  waiting for transfers between devices  124 us (66%)
  matrix products  20.9 us (11%)
  Pallas kernels  18 us (10%)
  blocking collectives  11.1 us (6%)
  starting transfers between devices  10.3 us (5%)
  other arithmetic  2.73 us (1%)
    all_to_all x1, waiting for transfers between devices, on_device(): lax.all_to_all(slotted, 'fsdp', split_axis=0, concat_axis=0, tiled=True)  71.2 us
    all_to_all x1, waiting for transfers between devices, on_device(): lax.all_to_all(scaled, 'fsdp', split_axis=0, concat_axis=0, tiled=True)  53.2 us
    dot_general x1, matrix products, on_device(): lax.dot_general(columns, block, (((0,), (0,)), ((), ())), preferred_eleme...  12.4 us
    all_to_all x1, blocking collectives, on_device(): lax.all_to_all(message, 'fsdp', split_axis=0, concat_axis=0, tiled=True)  11.1 us
    pallas_call x1, Pallas kernels, precondition(): pl.pallas_call(precond_kernel, out_shape=(pltpu.VMEM((height, width), jnp...  10.7 us
    dot_general x1, matrix products, on_device(): left_gram = jnp.dot(rows, block.T, preferred_element_type=jnp.float32)  8.47 us
    all_to_all x1, starting transfers between devices, on_device(): lax.all_to_all(slotted, 'fsdp', split_axis=0, concat_axis=0, tiled=True)  7.33 us
  transfers between devices with their start and end apart: 2, of which 2 were waited for; matrix products, arithmetic and copies ran while one was open for 13% of the time, Pallas kernels for 0%

profile of v3, /device:TPU:0, one launch (start us, length us, event | category | flops | bytes accessed | tf_op | source)
XLA Modules:
  0.0 188.5 jit_solution(6763081746375037784)
XLA Ops:
  0.6 0.0 copy-start.1
  0.6 0.0 copy-start
  0.7 3.1 %pack.1 = bf16[32,40,1280]{2,1,0:T(8,128)(2,1)} custom-call(s32[24]{0:T(128)} %owners.1, bf16[24,40,1280]{2,1,0:T(8,128)(2,1)} %bitcast.27), custom_call_target="tpu_custom_call" | custom-call | bytes 6553600 | tf_op jit(solution)/shard_map/pack/pallas_call | solution.py:52
  3.7 7.3 %all-to-all-start = ((bf16[32,40,1280]{2,1,0:T(8,128)(2,1)}), bf16[32,40,1280]{2,1,0:T(8,128)(2,1)S(1)}, u32[]{:S(2)}, u32[]{:S(2)}) async-start(bf16[32,40,1280]{2,1,0:T(8,128)(2,1)} %pack.1), calls=%async_computation | async-start | bytes 6553600 | tf_op jit(solution)/shard_map/all_to_all | solution.py:196
  11.1 0.0 copy-done.1
  11.1 0.1 copy.12
  11.2 0.2 reduce-window.8
  11.4 0.1 reduce
  11.5 0.0 copy-done
  11.5 2.3 %multiply_reduce_fusion = f32[24]{0:T(128)S(1)} fusion(bf16[1,24,40,1280]{3,2,1,0:T(8,128)(2,1)} %param.7), kind=kLoop, calls=%fused_computation.6 | loop fusion | flops 3686376 | bytes 2457696 | tf_op jit(solution)/shard_map/reduce_sum | solution.py:206
  13.9 0.1 convert_reduce_fusion
  14.0 71.2 %all-to-all-done = bf16[32,40,1280]{2,1,0:T(8,128)(2,1)S(1)} async-done(((bf16[32,40,1280]{2,1,0:T(8,128)(2,1)}), bf16[32,40,1280]{2,1,0:T(8,128)(2,1)S(1)}, u32[]{:S(2)}, u32[]{:S(2)}) %all-to-all-start) | async-done | bytes 3276832 | tf_op jit(solution)/shard_map/all_to_all | solution.py:196
  85.2 10.7 %precondition.1 = (f32[1280,1280]{1,0:T(8,128)S(1)}, f32[32,2,128]{2,1,0:T(2,128)S(1)}, bf16[1280,1280]{1,0:T(8,128)(2,1)}) custom-call(bf16[1280,1280]{1,0:T(8,128)(2,1)} %bitcast.28, bf16[1280,1280]{1,0:T(8,128)(2,1)S(1)} %bitcast.22, bf16[1280,1280]{1,0:T(8,128)(2,1)} %bitcast.29, f32[1,128]{1,0:T(1,128)S(1)} %bitcast.25, f32[1,128]{1,0:T(1,128)S(1)} %bitcast.23), custom_call_target="tpu_custom_call" | custom-call | flops 8388608000 | bytes 19660800 | tf_op jit(solution)/shard_map/precondition/pallas_call | solution.py:133
  96.0 11.1 %all_to_all.15.sums = f32[32,2,128]{2,1,0:T(2,128)S(1)} all-to-all(f32[32,2,128]{2,1,0:T(2,128)S(1)} %get-tuple-element.7), channel_id=1, replica_groups=mesh['rep'=1,'fsdp'=32] {'fsdp'}, dimensions={0} | all-to-all | bytes 65536 | tf_op jit(solution)/shard_map/all_to_all | solution.py:214
  107.1 2.0 %graft.1 = bf16[1280,1280]{1,0:T(8,128)(2,1)} custom-call(f32[32,2,128]{2,1,0:T(2,128)S(1)} %all_to_all.15.sums, f32[1,128]{1,0:T(1,128)S(1)} %bitcast.24, f32[1280,1280]{1,0:T(8,128)S(1)} %get-tuple-element.8.precond), custom_call_target="tpu_custom_call" | custom-call | flops 1638400 | bytes 9830400 | tf_op jit(solution)/shard_map/graft/pallas_call | solution.py:173
  109.1 3.0 %all-to-all-start.2 = ((bf16[32,40,1280]{2,1,0:T(8,128)(2,1)}), bf16[32,40,1280]{2,1,0:T(8,128)(2,1)S(1)}, u32[]{:S(2)}, u32[]{:S(2)}) async-start(bf16[32,40,1280]{2,1,0:T(8,128)(2,1)} %bitcast.26), calls=%async_computation.2 | async-start | bytes 6553600 | tf_op jit(solution)/shard_map/all_to_all | solution.py:218
  112.1 0.0 copy-start.2
  112.1 12.4 %fusion.2 = f32[1,1280,1280]{2,1,0:T(8,128)} fusion(bf16[1280,1280]{1,0:T(8,128)(2,1)} %get-tuple-element.6, f32[1,1280,1280]{2,1,0:T(8,128)} %param.11), kind=kOutput, calls=%fused_computation.4 | convolution fusion | flops 4199219200 | bytes 16384000 | tf_op jit(solution)/shard_map/dot_general | solution.py:225
  124.5 0.0 copy-done.2
  124.5 8.5 %fusion.3 = f32[1,1280,1280]{2,1,0:T(8,128)} fusion(bf16[1280,1280]{1,0:T(8,128)(2,1)S(1)} %copy-done.2, f32[1,1280,1280]{2,1,0:T(8,128)} %param.10), kind=kOutput, calls=%fused_computation.5 | convolution fusion | flops 4199219200 | bytes 16384000 | tf_op jit(solution)/shard_map/dot_general | solution.py:224
  133.0 53.2 %all-to-all-done.2.returned = bf16[32,40,1280]{2,1,0:T(8,128)(2,1)S(1)} async-done(((bf16[32,40,1280]{2,1,0:T(8,128)(2,1)}), bf16[32,40,1280]{2,1,0:T(8,128)(2,1)S(1)}, u32[]{:S(2)}, u32[]{:S(2)}) %all-to-all-start.2) | async-done | bytes 3276832 | tf_op jit(solution)/shard_map/all_to_all | solution.py:218
  186.2 2.2 %unpack.1 = bf16[24,40,1280]{2,1,0:T(8,128)(2,1)} custom-call(s32[24]{0:T(128)S(1)} %copy-done, bf16[32,40,1280]{2,1,0:T(8,128)(2,1)S(1)} %all-to-all-done.2.returned), custom_call_target="tpu_custom_call" | custom-call | bytes 4915200 | tf_op jit(solution)/shard_map/unpack/pallas_call | solution.py:83
  (3 shorter events, 0.0 us)
Async XLA Ops:
  0.6 10.5 %copy-start.1 = (s32[2]{0:T(128)S(1)}, s32[2]{0:T(128)}, u32[]{:S(2)}) copy-start(s32[2]{0:T(128)} %param.8) | copy-start | bytes 28
  0.6 10.9 %copy-start = (s32[24]{0:T(128)S(1)}, s32[24]{0:T(128)}, u32[]{:S(2)}) copy-start(s32[24]{0:T(128)} %owners.1) | copy-start | bytes 292
  3.7 81.5 %all-to-all-start = ((bf16[32,40,1280]{2,1,0:T(8,128)(2,1)}), bf16[32,40,1280]{2,1,0:T(8,128)(2,1)S(1)}, u32[]{:S(2)}, u32[]{:S(2)}) async-start(bf16[32,40,1280]{2,1,0:T(8,128)(2,1)} %pack.1), calls=%async_computation | async-start | bytes 6553600 | tf_op jit(solution)/shard_map/all_to_all | solution.py:196
  109.1 77.1 %all-to-all-start.2 = ((bf16[32,40,1280]{2,1,0:T(8,128)(2,1)}), bf16[32,40,1280]{2,1,0:T(8,128)(2,1)S(1)}, u32[]{:S(2)}, u32[]{:S(2)}) async-start(bf16[32,40,1280]{2,1,0:T(8,128)(2,1)} %bitcast.26), calls=%async_computation.2 | async-start | bytes 6553600 | tf_op jit(solution)/shard_map/all_to_all | solution.py:218
  112.1 12.4 %copy-start.2 = (bf16[1280,1280]{1,0:T(8,128)(2,1)S(1)}, bf16[1280,1280]{1,0:T(8,128)(2,1)}, u32[]{:S(2)}) copy-start(bf16[1280,1280]{1,0:T(8,128)(2,1)} %get-tuple-element.6) | copy-start | bytes 9830404
